TPU v7x, 32 devices: a whole 2x2x4 slice. The times are simulated.
32 devices in a mesh: seq: 8 (over y, x, core), rep: 4 (over z).
Axes of the slice: x: 2, y: 2, z: 4, core: 2. Of those that a mesh axis runs over, the one named last changes fastest.
Arguments:
- query_rows: bfloat16 [8, 8, 256, 1152], P('rep', 'seq'), as said below
- key_rows: bfloat16 [8, 8, 256, 1152], P('rep', 'seq'), as said below
- value_rows: bfloat16 [8, 8, 256, 1152], P('rep', 'seq'), may hold values from -6 to 6
- out_grad: bfloat16 [8, 8, 256, 1152], P('rep', 'seq'), may hold values from -6 to 6
- out_weight: bfloat16 [1152, 1152], replicated, may hold values from -0.1875 to 0.1875
- frame_count: int32 [8], P('rep'), may hold values from 1 to 8, as said below
- pos_count: int32 [8], P('rep'), may hold values from 64 to 256, as said below
Outputs:
- projected: bfloat16 [8, 8, 256, 1152], P('rep', 'seq')
- grad_query: bfloat16 [8, 8, 256, 1152], P('rep', 'seq')
- grad_key: bfloat16 [8, 8, 256, 1152], P('rep', 'seq')
- grad_value: bfloat16 [8, 8, 256, 1152], P('rep', 'seq')
- grad_weight: float32 [1152, 1152], P('seq')
Inputs may be any that keep to these rules, and one draw needn't show every extreme that they name: `query_rows`: entries lie within -40 to 40. `key_rows`: entries lie within -40 to 40. `frame_count`: some clip has all 8 frames live. `pos_count`: some clip has all 256 positions live.
All inputs are finite; a program needn't handle non-finite values.
Results may differ from a plain program's by a relative error of at most 0.0057.
Values may be sent and summed in bfloat16 or wider, within the bound.
No kernel may reach another device: no remote copies, remote signals or barrier semaphores. Data moves between devices by JAX's collectives and lax.ppermute only.
A program may use at most 128 MiB of HBM per device.

v0:
```python
import math
import jax
import jax.numpy as jnp
from jax import lax
from jax.sharding import PartitionSpec as P

HEADS = 16


def attend_local(query_part, key_part, value_part, key_live, row_live):
    nframe, npos_part, width = query_part.shape
    head_dim = width // HEADS
    inv_root = 1.0 / math.sqrt(head_dim)
    shape_heads = (nframe, npos_part, HEADS, head_dim)
    query_heads = query_part.reshape(shape_heads)
    key_heads = key_part.reshape(shape_heads)
    value_heads = value_part.reshape(shape_heads)
    scores = (
        jnp.einsum("fphd,tphd->phft", query_heads, key_heads, preferred_element_type=jnp.float32)
        * inv_root
    )
    scores = jnp.where(key_live, scores, -1e30)
    highest = jnp.max(scores, axis=-1, keepdims=True)
    expo = jnp.exp(scores - highest) * key_live.astype(jnp.float32)
    weights = expo / jnp.sum(expo, axis=-1, keepdims=True)
    rounded = weights.astype(jnp.bfloat16)
    mixed = jnp.einsum("phft,tphd->fphd", rounded, value_heads, preferred_element_type=jnp.float32)
    attn_out = jnp.where(row_live[:, :, None], mixed.reshape(nframe, npos_part, width), 0.0).astype(
        jnp.bfloat16
    )
    return (attn_out, weights, rounded)


def attend_back(query_part, key_part, value_part, cot_part, weights, rounded):
    nframe, npos_part, width = query_part.shape
    head_dim = width // HEADS
    inv_root = 1.0 / math.sqrt(head_dim)
    shape_heads = (nframe, npos_part, HEADS, head_dim)
    cot_heads = cot_part.reshape(shape_heads)
    value_heads = value_part.reshape(shape_heads)
    grad_value = jnp.einsum(
        "phft,fphd->tphd", rounded, cot_heads, preferred_element_type=jnp.float32
    )
    grad_attn = jnp.einsum(
        "fphd,tphd->phft", cot_heads, value_heads, preferred_element_type=jnp.float32
    )
    row_delta = jnp.sum(weights * grad_attn, axis=-1, keepdims=True)
    grad_score = weights * (grad_attn - row_delta) * inv_root
    key_wide = key_part.astype(jnp.float32).reshape(shape_heads)
    query_wide = query_part.astype(jnp.float32).reshape(shape_heads)
    grad_query = jnp.einsum(
        "phft,tphd->fphd", grad_score, key_wide, precision=lax.Precision.HIGHEST
    )
    grad_key = jnp.einsum(
        "phft,fphd->tphd", grad_score, query_wide, precision=lax.Precision.HIGHEST
    )
    full = (nframe, npos_part, width)
    return (
        grad_query.reshape(full).astype(jnp.bfloat16),
        grad_key.reshape(full).astype(jnp.bfloat16),
        grad_value.reshape(full).astype(jnp.bfloat16),
    )


def reduce_weight(flat_grad, flat_out):
    mine = lax.psum_scatter(
        lax.dot_general(
            flat_grad, flat_out, (((0,), (0,)), ((), ())), preferred_element_type=jnp.float32
        ),
        "seq",
        scatter_dimension=0,
        tiled=True,
    )
    return lax.psum(mine, "rep")


def shards(query_rows, key_rows, value_rows, out_grad, out_weight, frame_count, pos_count):
    clip_local, frame_local, npos_all, width = query_rows.shape
    rank = lax.axis_index("seq")
    query_pos, key_pos, value_pos = (
        lax.all_to_all(query_rows, "seq", split_axis=2, concat_axis=1, tiled=True),
        lax.all_to_all(key_rows, "seq", split_axis=2, concat_axis=1, tiled=True),
        lax.all_to_all(value_rows, "seq", split_axis=2, concat_axis=1, tiled=True),
    )
    nframe = query_pos.shape[1]
    npos_part = query_pos.shape[2]
    frame_ids = jnp.arange(nframe, dtype=jnp.int32)
    position_ids = rank * npos_part + jnp.arange(npos_part, dtype=jnp.int32)
    key_live = frame_ids[None, :] < frame_count[:, None]
    row_live = key_live[:, :, None] & (position_ids[None, None, :] < pos_count[:, None, None])
    attn_pos, weights, rounded = jax.vmap(attend_local)(
        query_pos, key_pos, value_pos, key_live, row_live
    )
    attn_frames = lax.all_to_all(attn_pos, "seq", split_axis=1, concat_axis=2, tiled=True)
    flat_out = attn_frames.reshape(-1, width)
    flat_grad = out_grad.reshape(-1, width)
    projected = lax.dot_general(
        flat_out, out_weight, (((1,), (1,)), ((), ())), preferred_element_type=jnp.float32
    )
    projected = projected.astype(jnp.bfloat16).reshape(query_rows.shape)
    own_frames = rank * frame_local + jnp.arange(frame_local, dtype=jnp.int32)
    frame_alive = own_frames[None, :, None] < frame_count[:, None, None]
    place_alive = jnp.arange(npos_all, dtype=jnp.int32)[None, None, :] < pos_count[:, None, None]
    out_cot = jnp.dot(flat_grad, out_weight, preferred_element_type=jnp.float32).reshape(
        query_rows.shape
    )
    out_cot = jnp.where((frame_alive & place_alive)[..., None], out_cot, 0.0).astype(jnp.bfloat16)
    cot_pos = lax.all_to_all(out_cot, "seq", split_axis=2, concat_axis=1, tiled=True)
    grad_query_pos, grad_key_pos, grad_value_pos = jax.vmap(attend_back)(
        query_pos, key_pos, value_pos, cot_pos, weights, rounded
    )
    grad_query, grad_key, grad_value = (
        lax.all_to_all(grad_query_pos, "seq", split_axis=1, concat_axis=2, tiled=True),
        lax.all_to_all(grad_key_pos, "seq", split_axis=1, concat_axis=2, tiled=True),
        lax.all_to_all(grad_value_pos, "seq", split_axis=1, concat_axis=2, tiled=True),
    )
    grad_weight = reduce_weight(flat_grad, flat_out)
    return (projected, grad_query, grad_key, grad_value, grad_weight)


def solution(mesh):
    in_specs = (
        P("rep", "seq", None, None),
        P("rep", "seq", None, None),
        P("rep", "seq", None, None),
        P("rep", "seq", None, None),
        P(),
        P("rep"),
        P("rep"),
    )
    out_specs = (
        P("rep", "seq", None, None),
        P("rep", "seq", None, None),
        P("rep", "seq", None, None),
        P("rep", "seq", None, None),
        P("seq", None),
    )
    return jax.shard_map(shards, mesh=mesh, in_specs=in_specs, out_specs=out_specs, check_vma=False)
```

profile of v0, /device:TPU:0, one launch (start us, length us, event | category | flops | bytes accessed | tf_op | source)
XLA Modules:
  0.0 298.1 jit_solution(12987899901119479207)
XLA Ops:
  10.8 5.2 %all-to-all-start = ((bf16[2,1,256,1152]{3,0,1,2:T(2,128)(2,1)}), bf16[2,1,256,1152]{3,0,1,2:T(2,128)(2,1)}, u32[]{:S(2)}, u32[]{:S(2)}) async-start(bf16[2,1,256,1152]{3,0,1,2:T(2,128)(2,1)} %copy.97), calls=%async_computation | async-start | bytes 2359296 | tf_op jit(solution)/shard_map/all_to_all | solution.py:81
  19.5 13.4 %all-to-all-done = bf16[2,1,256,1152]{3,0,1,2:T(2,128)(2,1)} async-done(((bf16[2,1,256,1152]{3,0,1,2:T(2,128)(2,1)}), bf16[2,1,256,1152]{3,0,1,2:T(2,128)(2,1)}, u32[]{:S(2)}, u32[]{:S(2)}) %all-to-all-start) | async-done | bytes 1179680 | tf_op jit(solution)/shard_map/all_to_all | solution.py:81
  40.7 13.3 %all-to-all-done.1 = bf16[2,1,256,1152]{3,0,1,2:T(2,128)(2,1)} async-done(((bf16[2,1,256,1152]{3,0,1,2:T(2,128)(2,1)}), bf16[2,1,256,1152]{3,0,1,2:T(2,128)(2,1)}, u32[]{:S(2)}, u32[]{:S(2)}) %all-to-all-start.1) | async-done | bytes 1179680 | tf_op jit(solution)/shard_map/all_to_all | solution.py:82
  59.0 6.5 %reshape.214 = bf16[2,8,32,16,72]{4,3,0,2,1:T(8,128)(2,1)} reshape(bf16[2,1,256,1152]{3,0,1,2:T(2,128)(2,1)} %all-to-all-done) | data formatting | bytes 2359296 | tf_op jit(solution)/shard_map/vmap()/reshape | solution.py:15
  65.6 6.5 %reshape.215 = bf16[2,8,32,16,72]{4,3,0,2,1:T(8,128)(2,1)} reshape(bf16[2,1,256,1152]{3,0,1,2:T(2,128)(2,1)} %all-to-all-done.1) | data formatting | bytes 2359296 | tf_op jit(solution)/shard_map/vmap()/reshape | solution.py:16
  72.1 8.7 %fusion.38 = (f32[2,32,16,8]{3,2,1,0:T(8,128)S(1)}, f32[2,32,16,8,8]{3,4,2,1,0:T(8,128)}) fusion(f32[2,8]{1,0:T(2,128)S(1)} %get-tuple-element.31, pred[2,8]{1,0:T(4,128)(4,1)S(1)} %get-tuple-element.30, bf16[2,8,32,16,72]{4,3,0,2,1:T(8,128)(2,1)} %reshape.215, bf16[2,8,32,16,72]{4,3,0,2,1:T(8,128)(2,1)} %reshape.214), kind=kOutput, calls=%fused_computation.48 | convolution fusion | flops 9764871 | bytes 2654288 | tf_op jit(solution)/shard_map/vmap()/sub | solution.py:24
  80.8 6.5 %reshape.216 = bf16[2,8,32,16,72]{4,3,0,2,1:T(8,128)(2,1)} reshape(bf16[2,1,256,1152]{3,0,1,2:T(2,128)(2,1)} %all-to-all-done.2) | data formatting | bytes 2359296 | tf_op jit(solution)/shard_map/vmap()/reshape | solution.py:17
  93.1 4.6 %reshape.203 = bf16[2,8,32,1152]{3,2,1,0:T(8,128)(2,1)} reshape(bf16[2,8,32,16,72]{4,3,2,1,0:T(8,128)(2,1)} %copy.107) | data formatting | bytes 2359296 | tf_op jit(solution)/shard_map/vmap()/reshape | solution.py:28
  99.4 20.7 %all_to_all.81 = bf16[2,8,32,1152]{3,2,0,1:T(8,128)(2,1)S(1)} all-to-all(bf16[2,8,32,1152]{3,2,0,1:T(8,128)(2,1)S(1)} %copy.108), channel_id=1, replica_groups=mesh['seq'=8,'rep'=4] {'seq'}, dimensions={1} | all-to-all | bytes 2359296 | tf_op jit(solution)/shard_map/all_to_all | solution.py:94
  125.3 6.9 %copy.137 = f32[1152,1152]{1,0:T(8,128)} copy(f32[1152,1152]{0,1:T(8,128)} %convolution_bitcast_fusion) | data formatting | bytes 10616832
  136.7 19.9 %all_to_all.82 = bf16[2,1,256,1152]{3,0,1,2:T(2,128)(2,1)} all-to-all(bf16[2,1,256,1152]{3,0,1,2:T(2,128)(2,1)S(1)} %copy.110), channel_id=1, replica_groups=mesh['seq'=8,'rep'=4] {'seq'}, dimensions={2} | all-to-all | bytes 2359296 | tf_op jit(solution)/shard_map/all_to_all | solution.py:108
  156.5 6.5 %reshape.217 = bf16[2,8,32,16,72]{4,3,0,2,1:T(8,128)(2,1)} reshape(bf16[2,1,256,1152]{3,0,1,2:T(2,128)(2,1)} %all_to_all.82) | data formatting | bytes 2359296 | tf_op jit(solution)/shard_map/vmap()/reshape | solution.py:39
  163.0 4.7 %convert_bitcast_fusion = bf16[2,8,32,16,72]{4,1,3,2,0:T(8,128)(2,1)S(1)} fusion(bf16[2,8,32,16,72]{4,3,0,2,1:T(8,128)(2,1)} %reshape.217, f32[2,32,16,8,8]{3,4,2,1,0:T(8,128)} %get-tuple-element.33, f32[2,32,16,8]{3,2,1,0:T(8,128)S(1)} %get-tuple-element.32), kind=kOutput, calls=%fused_computation.14 | convolution fusion | flops 10158080 | bytes 2654208 | tf_op jit(solution)/shard_map/vmap(phft,fphd->tphd)/dot_general | solution.py:41
  169.5 4.6 %reshape.211 = bf16[2,8,32,1152]{3,2,0,1:T(8,128)(2,1)} reshape(bf16[2,8,32,16,72]{4,3,2,0,1:T(8,128)(2,1)} %copy.136) | data formatting | bytes 2359296 | tf_op jit(solution)/shard_map/vmap()/convert_element_type | solution.py:61
  174.2 4.5 %all-to-all-start.7 = ((bf16[2,8,32,1152]{3,2,0,1:T(8,128)(2,1)}), bf16[2,8,32,1152]{3,2,0,1:T(8,128)(2,1)}, u32[]{:S(2)}, u32[]{:S(2)}) async-start(bf16[2,8,32,1152]{3,2,0,1:T(8,128)(2,1)} %reshape.211), calls=%async_computation.7 | async-start | bytes 2359296 | tf_op jit(solution)/shard_map/all_to_all | solution.py:115
  178.6 9.1 %multiply_reduce_fusion = (f32[2,32,16,8]{3,2,1,0:T(8,128)S(1)}, f32[2,32,16,8,8]{3,4,2,1,0:T(8,128)}) fusion(f32[2,32,16,8,8]{3,4,2,1,0:T(8,128)} %get-tuple-element.33, f32[2,32,16,8]{3,2,1,0:T(8,128)S(1)} %get-tuple-element.32, bf16[2,8,32,16,72]{4,3,0,2,1:T(8,128)(2,1)} %reshape.216, bf16[2,8,32,16,72]{4,3,0,2,1:T(8,128)(2,1)} %reshape.217), kind=kOutput, calls=%fused_computation.3 | convolution fusion | flops 9625600 | bytes 2949120 | tf_op jit(solution)/shard_map/vmap(fphd,tphd->phft)/dot_general | solution.py:44
  187.7 7.4 %convert_bitcast_fusion.1 = bf16[2,8,32,16,72]{4,1,3,2,0:T(8,128)(2,1)S(1)} fusion(bf16[2,8,32,16,72]{4,3,0,2,1:T(8,128)(2,1)S(1)} %copy-done.3, f32[2,32,16,8,8]{3,4,2,1,0:T(8,128)} %get-tuple-element.35, f32[2,32,16,8]{3,2,1,0:T(8,128)S(1)} %get-tuple-element.34, f32[2,32,16,8,8]{3,4,2,1,0:T(8,128)S(1)} %copy-done.7, ...), kind=kOutput, calls=%fused_computation.15 | convolution fusion | flops 57475072 | bytes 2949120 | tf_op jit(solution)/shard_map/vmap(phft,fphd->tphd)/dot_general | solution.py:54
  197.0 4.6 %reshape.210 = bf16[2,8,32,1152]{3,2,0,1:T(8,128)(2,1)} reshape(bf16[2,8,32,16,72]{4,3,2,0,1:T(8,128)(2,1)} %copy.135) | data formatting | bytes 2359296 | tf_op jit(solution)/shard_map/vmap()/convert_element_type | solution.py:60
  201.6 4.5 %all-to-all-start.6 = ((bf16[2,8,32,1152]{3,2,0,1:T(8,128)(2,1)}), bf16[2,8,32,1152]{3,2,0,1:T(8,128)(2,1)}, u32[]{:S(2)}, u32[]{:S(2)}) async-start(bf16[2,8,32,1152]{3,2,0,1:T(8,128)(2,1)} %reshape.210), calls=%async_computation.6 | async-start | bytes 2359296 | tf_op jit(solution)/shard_map/all_to_all | solution.py:114
  206.1 8.3 %convert_bitcast_fusion.2 = bf16[2,8,32,16,72]{4,1,3,2,0:T(8,128)(2,1)S(1)} fusion(bf16[2,8,32,16,72]{4,3,0,2,1:T(8,128)(2,1)} %reshape.215, f32[2,32,16,8,8]{3,4,2,1,0:T(8,128)} %get-tuple-element.35, f32[2,32,16,8]{3,2,1,0:T(8,128)} %copy-done.8, f32[2,32,16,8,8]{3,4,2,1,0:T(8,128)} %get-tuple-element.33, f32[2,32,16,8]{3,2,1,0:T(8,128)S(1)} %get-tuple-element.32), kind=kOutput, calls=%fused_computation.16 | convolution fusion | flops 57475072 | bytes 2949120 | tf_op jit(solution)/shard_map/vmap(phft,tphd->fphd)/dot_general | solution.py:51
  216.2 4.6 %reshape.209 = bf16[2,8,32,1152]{3,2,0,1:T(8,128)(2,1)} reshape(bf16[2,8,32,16,72]{4,3,2,0,1:T(8,128)(2,1)} %copy.134) | data formatting | bytes 2359296 | tf_op jit(solution)/shard_map/vmap()/convert_element_type | solution.py:59
  222.9 4.3 %all-to-all-start.5 = ((bf16[2,8,32,1152]{3,2,0,1:T(8,128)(2,1)}), bf16[2,8,32,1152]{3,2,0,1:T(8,128)(2,1)}, u32[]{:S(2)}, u32[]{:S(2)}) async-start(bf16[2,8,32,1152]{3,2,0,1:T(8,128)(2,1)} %reshape.209), calls=%async_computation.5 | async-start | bytes 2359296 | tf_op jit(solution)/shard_map/all_to_all | solution.py:113
  234.6 9.5 %all-to-all-done.5 = bf16[2,8,32,1152]{3,2,0,1:T(8,128)(2,1)} async-done(((bf16[2,8,32,1152]{3,2,0,1:T(8,128)(2,1)}), bf16[2,8,32,1152]{3,2,0,1:T(8,128)(2,1)}, u32[]{:S(2)}, u32[]{:S(2)}) %all-to-all-start.5) | async-done | bytes 1179680 | tf_op jit(solution)/shard_map/all_to_all | solution.py:113
  249.4 39.1 %all-reduce.2.cloned.1.call-done = f32[144,1152]{0,1:T(8,128)} async-done(((f32[144,1152]{0,1:T(8,128)}), f32[144,1152]{0,1:T(8,128)}) %all-reduce.2.cloned.1.call-update) | async-done | bytes 663568 | tf_op jit(solution)/shard_map/psum | solution.py:74
  (54 shorter events, 59.9 us)
Async XLA Ops:
  7.2 125.2 %copy-start = (bf16[1152,1152]{1,0:T(8,128)(2,1)S(1)}, bf16[1152,1152]{1,0:T(8,128)(2,1)}, u32[]{:S(2)}) copy-start(bf16[1152,1152]{1,0:T(8,128)(2,1)} %param.11) | copy-start | bytes 7962628
  10.8 22.1 %all-to-all-start = ((bf16[2,1,256,1152]{3,0,1,2:T(2,128)(2,1)}), bf16[2,1,256,1152]{3,0,1,2:T(2,128)(2,1)}, u32[]{:S(2)}, u32[]{:S(2)}) async-start(bf16[2,1,256,1152]{3,0,1,2:T(2,128)(2,1)} %copy.97), calls=%async_computation | async-start | bytes 2359296 | tf_op jit(solution)/shard_map/all_to_all | solution.py:81
  32.9 21.1 %all-to-all-start.1 = ((bf16[2,1,256,1152]{3,0,1,2:T(2,128)(2,1)}), bf16[2,1,256,1152]{3,0,1,2:T(2,128)(2,1)}, u32[]{:S(2)}, u32[]{:S(2)}) async-start(bf16[2,1,256,1152]{3,0,1,2:T(2,128)(2,1)} %copy.99), calls=%async_computation.1 | async-start | bytes 2359296 | tf_op jit(solution)/shard_map/all_to_all | solution.py:82
  37.2 21.6 %copy-start.6 = (s32[2]{0:T(128)S(1)}, s32[2]{0:T(128)}, u32[]{:S(2)}) copy-start(s32[2]{0:T(128)} %param.13) | copy-start | bytes 28
  37.2 21.7 %copy-start.5 = (s32[2]{0:T(128)S(1)}, s32[2]{0:T(128)}, u32[]{:S(2)}) copy-start(s32[2]{0:T(128)} %param.12) | copy-start | bytes 28
  54.0 26.8 %all-to-all-start.2 = ((bf16[2,1,256,1152]{3,0,1,2:T(2,128)(2,1)}), bf16[2,1,256,1152]{3,0,1,2:T(2,128)(2,1)}, u32[]{:S(2)}, u32[]{:S(2)}) async-start(bf16[2,1,256,1152]{3,0,1,2:T(2,128)(2,1)} %copy.103), calls=%async_computation.2 | async-start | bytes 2359296 | tf_op jit(solution)/shard_map/all_to_all | solution.py:83
  58.2 169.0 %reduce-scatter.4.cloned.1.call-start = ((), (), s32[]{:S(2)}) async-start(), calls=%async_computation.10 | async-start | bytes 5971968
  99.4 21.8 %copy-start.4 = (bf16[2,1,256,1152]{3,2,1,0:T(8,128)(2,1)S(1)}, bf16[2,1,256,1152]{3,2,1,0:T(8,128)(2,1)}, u32[]{:S(2)}) copy-start(bf16[2,1,256,1152]{3,2,1,0:T(8,128)(2,1)} %param.10) | copy-start | bytes 3538948
  120.2 1.0 copy-start.1
  174.2 27.5 %all-to-all-start.7 = ((bf16[2,8,32,1152]{3,2,0,1:T(8,128)(2,1)}), bf16[2,8,32,1152]{3,2,0,1:T(8,128)(2,1)}, u32[]{:S(2)}, u32[]{:S(2)}) async-start(bf16[2,8,32,1152]{3,2,0,1:T(8,128)(2,1)} %reshape.211), calls=%async_computation.7 | async-start | bytes 2359296 | tf_op jit(solution)/shard_map/all_to_all | solution.py:115
  178.6 9.1 %copy-start.3 = (bf16[2,8,32,16,72]{4,3,0,2,1:T(8,128)(2,1)S(1)}, bf16[2,8,32,16,72]{4,3,0,2,1:T(8,128)(2,1)}, u32[]{:S(2)}) copy-start(bf16[2,8,32,16,72]{4,3,0,2,1:T(8,128)(2,1)} %reshape.214) | copy-start | bytes 3538948
  178.6 9.1 %copy-start.7 = (f32[2,32,16,8,8]{3,4,2,1,0:T(8,128)S(1)}, f32[2,32,16,8,8]{3,4,2,1,0:T(8,128)}, u32[]{:S(2)}) copy-start(f32[2,32,16,8,8]{3,4,2,1,0:T(8,128)} %get-tuple-element.33) | copy-start | bytes 786436
  187.7 7.4 %copy-start.8 = (f32[2,32,16,8]{3,2,1,0:T(8,128)}, f32[2,32,16,8]{3,2,1,0:T(8,128)S(1)}, u32[]{:S(2)}) copy-start(f32[2,32,16,8]{3,2,1,0:T(8,128)S(1)} %get-tuple-element.34) | copy-start | bytes 98308
  201.6 21.3 %all-to-all-start.6 = ((bf16[2,8,32,1152]{3,2,0,1:T(8,128)(2,1)}), bf16[2,8,32,1152]{3,2,0,1:T(8,128)(2,1)}, u32[]{:S(2)}, u32[]{:S(2)}) async-start(bf16[2,8,32,1152]{3,2,0,1:T(8,128)(2,1)} %reshape.210), calls=%async_computation.6 | async-start | bytes 2359296 | tf_op jit(solution)/shard_map/all_to_all | solution.py:114
  222.9 21.1 %all-to-all-start.5 = ((bf16[2,8,32,1152]{3,2,0,1:T(8,128)(2,1)}), bf16[2,8,32,1152]{3,2,0,1:T(8,128)(2,1)}, u32[]{:S(2)}, u32[]{:S(2)}) async-start(bf16[2,8,32,1152]{3,2,0,1:T(8,128)(2,1)} %reshape.209), calls=%async_computation.5 | async-start | bytes 2359296 | tf_op jit(solution)/shard_map/all_to_all | solution.py:113
  227.2 61.3 %all-reduce.2.cloned.1.call-start = ((), (), s32[]{:S(2)}) async-start(), calls=%async_computation.9 | async-start | bytes 2359296 | tf_op jit(solution)/shard_map/psum | solution.py:74
  244.0 2.5 copy-start.2
Sparse Core Ops, SparseCore 0:
  132.3 65.9 reduce-scatter.3
  230.4 58.0 all-reduce.1
where the time goes:
time: 303 us; the launch traced here: 298 us
  local copies, waits for them, and re-layouts  83.8 us (28%)
  waiting for transfers between devices  77.4 us (26%)
  matrix products  52.4 us (17%)
  blocking collectives  40.6 us (13%)
  starting transfers between devices  27.5 us (9%)
  between operations  14.5 us (5%)
    psum x1, waiting for transfers between devices, reduce_weight(): return lax.psum(mine, 'rep')  39.1 us
    unnamed x24, local copies, waits for them, and re-layouts  23.5 us
    all_to_all x1, blocking collectives, shards(): lax.all_to_all(attn_pos, 'seq', split_axis=1, concat_axis=2, tiled=True)  20.7 us
    all_to_all x1, blocking collectives, shards(): lax.all_to_all(out_cot, 'seq', split_axis=2, concat_axis=1, tiled=True)  19.9 us
    all_to_all x1, waiting for transfers between devices, shards(): lax.all_to_all(query_rows, 'seq', split_axis=2, concat_axis=1, tiled=True)  13.4 us
    all_to_all x1, waiting for transfers between devices, shards(): lax.all_to_all(key_rows, 'seq', split_axis=2, concat_axis=1, tiled=True)  13.3 us
    all_to_all x1, waiting for transfers between devices, shards(): lax.all_to_all(grad_query_pos, 'seq', split_axis=1, concat_axis=2, tiled=...  9.45 us
    dot_general x1, matrix products, attend_back(): jnp.einsum('fphd,tphd->phft', cot_heads, value_heads, preferred_element_t...  9.06 us
  transfers between devices with their start and end apart: 8, of which 5 were waited for; matrix products, arithmetic and copies ran while one was open for 34% of the time, Pallas kernels for 0%

commit v1 on v0

--- a/solution.py
+++ b/solution.py
@@ -105,7 +105,10 @@
         query_rows.shape
     )
     out_cot = jnp.where((frame_alive & place_alive)[..., None], out_cot, 0.0).astype(jnp.bfloat16)
-    cot_pos = lax.all_to_all(out_cot, "seq", split_axis=2, concat_axis=1, tiled=True)
+    cot_pos = jnp.concatenate(
+        lax.all_to_all(jnp.stack(jnp.split(out_cot, lax.axis_size("seq"), axis=2)), "seq", 0, 0),
+        axis=1,
+    )
     grad_query_pos, grad_key_pos, grad_value_pos = jax.vmap(attend_back)(
         query_pos, key_pos, value_pos, cot_pos, weights, rounded
     )

time: 303 us -> 334 us (1.10)
  waiting for transfers between devices: 77.4 us -> 95.8 us
  blocking collectives: 40.6 us -> 24.3 us
  local copies, waits for them, and re-layouts: 83.8 us -> 96.9 us
  matrix products: 52.4 us -> 64 us
  starting transfers between devices: 27.5 us -> 31.4 us
    all_to_all x2 -> x1, blocking collectives: 40.6 us -> 24.3 us  [shards(): lax.all_to_all(jnp.stack(jnp.split(out_cot, lax.axis_size('seq'), axis=2)...]
    all_to_all x0 -> x1, waiting for transfers between devices: none -> 12 us  [shards(): lax.all_to_all(attn_pos, 'seq', split_axis=1, concat_axis=2, tiled=True)]
    unnamed x24 -> x31, local copies, waits for them, and re-layouts: 23.5 us -> 34.7 us
    dot_general x1, matrix products: 4.07 us -> 14.7 us  [attend_local(): jnp.einsum('phft,tphd->fphd', rounded, value_heads, preferred_element_typ...]
    all_to_all x1, waiting for transfers between devices: 0.01 us -> 9.43 us  [shards(): lax.all_to_all(grad_value_pos, 'seq', split_axis=1, concat_axis=2, tiled=...]
    another operation x0 -> x2, local copies, waits for them, and re-layouts: none -> 7.39 us  [the longest x1 5.79 us: attend_back(): cot_heads = cot_part.reshape(shape_heads)]
    reshape x1 -> x0, local copies, waits for them, and re-layouts: 6.53 us -> none  [attend_back(): cot_heads = cot_part.reshape(shape_heads)]
    all_to_all x0 -> x1, starting transfers between devices: none -> 4.26 us  [shards(): lax.all_to_all(attn_pos, 'seq', split_axis=1, concat_axis=2, tiled=True)]
  transfers between devices with their start and end apart: 8 -> 9, of which waited for: 5 -> 7; matrix products, arithmetic and copies ran while one was open for 34% -> 34% of each run, Pallas kernels for 0% -> 0%
where the time goes in v1:
time: 334 us; the launch traced here: 329 us
  local copies, waits for them, and re-layouts  96.9 us (29%)
  waiting for transfers between devices  95.8 us (29%)
  matrix products  64 us (19%)
  starting transfers between devices  31.4 us (9%)
  blocking collectives  24.3 us (7%)
  between operations  14.4 us (4%)
    psum x1, waiting for transfers between devices, reduce_weight(): return lax.psum(mine, 'rep')  40.1 us
    unnamed x31, local copies, waits for them, and re-layouts  34.7 us
    all_to_all x1, blocking collectives, shards(): lax.all_to_all(jnp.stack(jnp.split(out_cot, lax.axis_size('seq'), axis=2)...  24.3 us
    dot_general x1, matrix products, attend_local(): jnp.einsum('phft,tphd->fphd', rounded, value_heads, preferred_element_typ...  14.7 us
    all_to_all x1, waiting for transfers between devices, shards(): lax.all_to_all(query_rows, 'seq', split_axis=2, concat_axis=1, tiled=True)  13.4 us
    all_to_all x1, waiting for transfers between devices, shards(): lax.all_to_all(key_rows, 'seq', split_axis=2, concat_axis=1, tiled=True)  13 us
    all_to_all x1, waiting for transfers between devices, shards(): lax.all_to_all(attn_pos, 'seq', split_axis=1, concat_axis=2, tiled=True)  12 us
    all_to_all x1, waiting for transfers between devices, shards(): lax.all_to_all(grad_value_pos, 'seq', split_axis=1, concat_axis=2, tiled=...  9.43 us
  transfers between devices with their start and end apart: 9, of which 7 were waited for; matrix products, arithmetic and copies ran while one was open for 34% of the time, Pallas kernels for 0%

profile of v1, /device:TPU:0, one launch (start us, length us, event | category | flops | bytes accessed | tf_op | source)
XLA Modules:
  0.0 328.6 jit_solution(11182204355906068811)
XLA Ops:
  10.8 5.2 %all-to-all-start = ((bf16[2,1,256,1152]{3,0,1,2:T(2,128)(2,1)}), bf16[2,1,256,1152]{3,0,1,2:T(2,128)(2,1)}, u32[]{:S(2)}, u32[]{:S(2)}) async-start(bf16[2,1,256,1152]{3,0,1,2:T(2,128)(2,1)} %copy.96), calls=%async_computation | async-start | bytes 2359296 | tf_op jit(solution)/shard_map/all_to_all | solution.py:81
  19.5 13.4 %all-to-all-done = bf16[2,1,256,1152]{3,0,1,2:T(2,128)(2,1)} async-done(((bf16[2,1,256,1152]{3,0,1,2:T(2,128)(2,1)}), bf16[2,1,256,1152]{3,0,1,2:T(2,128)(2,1)}, u32[]{:S(2)}, u32[]{:S(2)}) %all-to-all-start) | async-done | bytes 1179680 | tf_op jit(solution)/shard_map/all_to_all | solution.py:81
  40.9 13.0 %all-to-all-done.1 = bf16[2,1,256,1152]{3,0,1,2:T(2,128)(2,1)} async-done(((bf16[2,1,256,1152]{3,0,1,2:T(2,128)(2,1)}), bf16[2,1,256,1152]{3,0,1,2:T(2,128)(2,1)}, u32[]{:S(2)}, u32[]{:S(2)}) %all-to-all-start.1) | async-done | bytes 1179680 | tf_op jit(solution)/shard_map/all_to_all | solution.py:82
  54.0 4.6 %all-to-all-start.2 = ((bf16[2,1,256,1152]{3,0,1,2:T(2,128)(2,1)}), bf16[2,1,256,1152]{3,0,1,2:T(2,128)(2,1)}, u32[]{:S(2)}, u32[]{:S(2)}) async-start(bf16[2,1,256,1152]{3,0,1,2:T(2,128)(2,1)} %copy.102), calls=%async_computation.2 | async-start | bytes 2359296 | tf_op jit(solution)/shard_map/all_to_all | solution.py:83
  62.8 6.5 %reshape.210 = bf16[2,8,32,16,72]{4,3,0,2,1:T(8,128)(2,1)} reshape(bf16[2,1,256,1152]{3,0,1,2:T(2,128)(2,1)} %all-to-all-done) | data formatting | bytes 2359296 | tf_op jit(solution)/shard_map/vmap()/reshape | solution.py:15
  69.4 6.5 %reshape.211 = bf16[2,8,32,16,72]{4,3,0,2,1:T(8,128)(2,1)} reshape(bf16[2,1,256,1152]{3,0,1,2:T(2,128)(2,1)} %all-to-all-done.1) | data formatting | bytes 2359296 | tf_op jit(solution)/shard_map/vmap()/reshape | solution.py:16
  75.9 8.6 %fusion.46 = (f32[2,32,16,8]{3,2,1,0:T(8,128)S(1)}, f32[2,32,16,8,8]{3,4,2,1,0:T(8,128)}) fusion(f32[2,8]{1,0:T(2,128)S(1)} %get-tuple-element.31, pred[2,8]{1,0:T(4,128)(4,1)S(1)} %get-tuple-element.30, bf16[2,8,32,16,72]{4,3,0,2,1:T(8,128)(2,1)} %reshape.211, bf16[2,8,32,16,72]{4,3,0,2,1:T(8,128)(2,1)} %reshape.210), kind=kOutput, calls=%fused_computation.64 | convolution fusion | flops 9764871 | bytes 2654288 | tf_op jit(solution)/shard_map/vmap()/sub | solution.py:24
  84.5 6.5 %reshape.212 = bf16[2,8,32,16,72]{4,3,0,2,1:T(8,128)(2,1)} reshape(bf16[2,1,256,1152]{3,0,1,2:T(2,128)(2,1)} %all-to-all-done.2) | data formatting | bytes 2359296 | tf_op jit(solution)/shard_map/vmap()/reshape | solution.py:17
  91.0 14.7 %convolution_bitcast_fusion.1 = bf16[2,8,32,16,72]{4,1,3,2,0:T(8,128)(2,1)S(1)} fusion(bf16[2,8,32,16,72]{4,3,0,2,1:T(8,128)(2,1)} %reshape.212, f32[2,32,16,8,8]{3,4,2,1,0:T(8,128)} %get-tuple-element.33, f32[2,32,16,8]{3,2,1,0:T(8,128)S(1)} %get-tuple-element.32), kind=kOutput, calls=%fused_computation.13 | convolution fusion | flops 9568256 | bytes 2654208 | tf_op jit(solution)/shard_map/vmap(phft,tphd->fphd)/dot_general | solution.py:27
  107.5 4.6 %reshape.199 = bf16[2,8,32,1152]{3,2,1,0:T(8,128)(2,1)} reshape(bf16[2,8,32,16,72]{4,3,2,1,0:T(8,128)(2,1)} %copy.106) | data formatting | bytes 2359296 | tf_op jit(solution)/shard_map/vmap()/reshape | solution.py:28
  123.9 12.0 %all-to-all-done.3 = bf16[2,8,32,1152]{3,2,0,1:T(8,128)(2,1)} async-done(((bf16[2,8,32,1152]{3,2,0,1:T(8,128)(2,1)}), bf16[2,8,32,1152]{3,2,0,1:T(8,128)(2,1)}, u32[]{:S(2)}, u32[]{:S(2)}) %all-to-all-start.3) | async-done | bytes 1179680 | tf_op jit(solution)/shard_map/all_to_all | solution.py:94
  142.4 6.9 %copy.134 = f32[1152,1152]{1,0:T(8,128)} copy(f32[1152,1152]{0,1:T(8,128)} %convolution_bitcast_fusion) | data formatting | bytes 10616832
  157.3 24.3 %all_to_all.77 = bf16[8,2,1,32,1152]{4,3,1,2,0:T(8,128)(2,1)} all-to-all(bf16[8,2,1,32,1152]{4,3,1,2,0:T(8,128)(2,1)} %fusion.33), channel_id=1, replica_groups=mesh['seq'=8,'rep'=4] {'seq'}, dimensions={0} | all-to-all | bytes 2359296 | tf_op jit(solution)/shard_map/all_to_all | solution.py:109
  181.5 5.8 %reshape_reshape.3 = bf16[2,8,32,16,72]{4,3,2,0,1:T(8,128)(2,1)} reshape(bf16[2,8,1,32,1152]{4,3,0,2,1:T(8,128)(2,1)} %bitcast.96) | data formatting | bytes 2359296 | tf_op jit(solution)/shard_map/vmap()/reshape;reshape | solution.py:39
  187.3 9.1 %multiply_reduce_fusion = (f32[2,32,16,8]{3,2,1,0:T(8,128)S(1)}, f32[2,32,16,8,8]{3,4,2,1,0:T(8,128)}) fusion(f32[2,32,16,8,8]{3,4,2,1,0:T(8,128)} %get-tuple-element.33, f32[2,32,16,8]{3,2,1,0:T(8,128)S(1)} %get-tuple-element.32, bf16[2,8,32,16,72]{4,3,0,2,1:T(8,128)(2,1)} %reshape.212, bf16[2,8,32,16,72]{4,3,2,0,1:T(8,128)(2,1)} %reshape_reshape.3), kind=kOutput, calls=%fused_computation.3 | convolution fusion | flops 9625600 | bytes 2949120 | tf_op jit(solution)/shard_map/vmap(fphd,tphd->phft)/dot_general | solution.py:44
  196.5 7.4 %convert_bitcast_fusion.1 = bf16[2,8,32,16,72]{4,1,3,2,0:T(8,128)(2,1)S(1)} fusion(bf16[2,8,32,16,72]{4,3,0,2,1:T(8,128)(2,1)S(1)} %copy-done.3, f32[2,32,16,8,8]{3,4,2,1,0:T(8,128)} %get-tuple-element.35, f32[2,32,16,8]{3,2,1,0:T(8,128)S(1)} %get-tuple-element.34, f32[2,32,16,8,8]{3,4,2,1,0:T(8,128)S(1)} %copy-done.7, ...), kind=kOutput, calls=%fused_computation.15 | convolution fusion | flops 57475072 | bytes 2949120 | tf_op jit(solution)/shard_map/vmap(phft,fphd->tphd)/dot_general | solution.py:54
  205.7 4.6 %reshape.206 = bf16[2,8,32,1152]{3,2,0,1:T(8,128)(2,1)} reshape(bf16[2,8,32,16,72]{4,3,2,0,1:T(8,128)(2,1)} %copy.132) | data formatting | bytes 2359296 | tf_op jit(solution)/shard_map/vmap()/convert_element_type | solution.py:60
  214.8 8.3 %convert_bitcast_fusion.2 = bf16[2,8,32,16,72]{4,1,3,2,0:T(8,128)(2,1)S(1)} fusion(bf16[2,8,32,16,72]{4,3,0,2,1:T(8,128)(2,1)} %reshape.211, f32[2,32,16,8,8]{3,4,2,1,0:T(8,128)} %get-tuple-element.35, f32[2,32,16,8]{3,2,1,0:T(8,128)} %copy-done.8, f32[2,32,16,8,8]{3,4,2,1,0:T(8,128)} %get-tuple-element.33, f32[2,32,16,8]{3,2,1,0:T(8,128)S(1)} %get-tuple-element.32), kind=kOutput, calls=%fused_computation.16 | convolution fusion | flops 57475072 | bytes 2949120 | tf_op jit(solution)/shard_map/vmap(phft,tphd->fphd)/dot_general | solution.py:51
  224.8 4.6 %reshape.205 = bf16[2,8,32,1152]{3,2,0,1:T(8,128)(2,1)} reshape(bf16[2,8,32,16,72]{4,3,2,0,1:T(8,128)(2,1)} %copy.131) | data formatting | bytes 2359296 | tf_op jit(solution)/shard_map/vmap()/convert_element_type | solution.py:59
  235.7 4.7 %convert_bitcast_fusion = bf16[2,8,32,16,72]{4,1,3,2,0:T(8,128)(2,1)S(1)} fusion(bf16[2,8,32,16,72]{4,3,2,0,1:T(8,128)(2,1)} %reshape_reshape.3, f32[2,32,16,8,8]{3,4,2,1,0:T(8,128)} %get-tuple-element.33, f32[2,32,16,8]{3,2,1,0:T(8,128)S(1)} %get-tuple-element.32), kind=kOutput, calls=%fused_computation.14 | convolution fusion | flops 10158080 | bytes 2654208 | tf_op jit(solution)/shard_map/vmap(phft,fphd->tphd)/dot_general | solution.py:41
  242.1 4.6 %reshape.207 = bf16[2,8,32,1152]{3,2,0,1:T(8,128)(2,1)} reshape(bf16[2,8,32,16,72]{4,3,2,0,1:T(8,128)(2,1)} %copy.133) | data formatting | bytes 2359296 | tf_op jit(solution)/shard_map/vmap()/convert_element_type | solution.py:61
  246.7 5.7 %all-to-all-done.5 = bf16[2,8,32,1152]{3,2,0,1:T(8,128)(2,1)} async-done(((bf16[2,8,32,1152]{3,2,0,1:T(8,128)(2,1)}), bf16[2,8,32,1152]{3,2,0,1:T(8,128)(2,1)}, u32[]{:S(2)}, u32[]{:S(2)}) %all-to-all-start.5) | async-done | bytes 1179680 | tf_op jit(solution)/shard_map/all_to_all | solution.py:116
  264.1 9.4 %all-to-all-done.7 = bf16[2,8,32,1152]{3,2,0,1:T(8,128)(2,1)} async-done(((bf16[2,8,32,1152]{3,2,0,1:T(8,128)(2,1)}), bf16[2,8,32,1152]{3,2,0,1:T(8,128)(2,1)}, u32[]{:S(2)}, u32[]{:S(2)}) %all-to-all-start.7) | async-done | bytes 1179680 | tf_op jit(solution)/shard_map/all_to_all | solution.py:118
  278.9 40.1 %all-reduce.2.cloned.1.call-done = f32[144,1152]{0,1:T(8,128)} async-done(((f32[144,1152]{0,1:T(8,128)}), f32[144,1152]{0,1:T(8,128)}) %all-reduce.2.cloned.1.call-update) | async-done | bytes 663568 | tf_op jit(solution)/shard_map/psum | solution.py:74
  (62 shorter events, 82.8 us)
Async XLA Ops:
  7.2 51.6 %copy-start = (bf16[1152,1152]{1,0:T(8,128)(2,1)S(1)}, bf16[1152,1152]{1,0:T(8,128)(2,1)}, u32[]{:S(2)}) copy-start(bf16[1152,1152]{1,0:T(8,128)(2,1)} %param.11) | copy-start | bytes 7962628
  10.8 22.1 %all-to-all-start = ((bf16[2,1,256,1152]{3,0,1,2:T(2,128)(2,1)}), bf16[2,1,256,1152]{3,0,1,2:T(2,128)(2,1)}, u32[]{:S(2)}, u32[]{:S(2)}) async-start(bf16[2,1,256,1152]{3,0,1,2:T(2,128)(2,1)} %copy.96), calls=%async_computation | async-start | bytes 2359296 | tf_op jit(solution)/shard_map/all_to_all | solution.py:81
  19.5 21.2 %copy-start.5 = (s32[2]{0:T(128)S(1)}, s32[2]{0:T(128)}, u32[]{:S(2)}) copy-start(s32[2]{0:T(128)} %param.12) | copy-start | bytes 28
  19.5 21.2 %copy-start.6 = (s32[2]{0:T(128)S(1)}, s32[2]{0:T(128)}, u32[]{:S(2)}) copy-start(s32[2]{0:T(128)} %param.13) | copy-start | bytes 28
  32.9 21.1 %all-to-all-start.1 = ((bf16[2,1,256,1152]{3,0,1,2:T(2,128)(2,1)}), bf16[2,1,256,1152]{3,0,1,2:T(2,128)(2,1)}, u32[]{:S(2)}, u32[]{:S(2)}) async-start(bf16[2,1,256,1152]{3,0,1,2:T(2,128)(2,1)} %copy.98), calls=%async_computation.1 | async-start | bytes 2359296 | tf_op jit(solution)/shard_map/all_to_all | solution.py:82
  54.0 30.5 %all-to-all-start.2 = ((bf16[2,1,256,1152]{3,0,1,2:T(2,128)(2,1)}), bf16[2,1,256,1152]{3,0,1,2:T(2,128)(2,1)}, u32[]{:S(2)}, u32[]{:S(2)}) async-start(bf16[2,1,256,1152]{3,0,1,2:T(2,128)(2,1)} %copy.102), calls=%async_computation.2 | async-start | bytes 2359296 | tf_op jit(solution)/shard_map/all_to_all | solution.py:83
  114.8 21.1 %all-to-all-start.3 = ((bf16[2,8,32,1152]{3,2,0,1:T(8,128)(2,1)}), bf16[2,8,32,1152]{3,2,0,1:T(8,128)(2,1)}, u32[]{:S(2)}, u32[]{:S(2)}) async-start(bf16[2,8,32,1152]{3,2,0,1:T(8,128)(2,1)} %copy.107), calls=%async_computation.3 | async-start | bytes 2359296 | tf_op jit(solution)/shard_map/all_to_all | solution.py:94
  119.1 137.7 %reduce-scatter.4.cloned.1.call-start = ((), (), s32[]{:S(2)}) async-start(), calls=%async_computation.10 | async-start | bytes 5971968
  135.9 2.5 copy-start.4
  137.3 1.0 copy-start.1
  187.3 9.2 %copy-start.3 = (bf16[2,8,32,16,72]{4,3,0,2,1:T(8,128)(2,1)S(1)}, bf16[2,8,32,16,72]{4,3,0,2,1:T(8,128)(2,1)}, u32[]{:S(2)}) copy-start(bf16[2,8,32,16,72]{4,3,0,2,1:T(8,128)(2,1)} %reshape.210) | copy-start | bytes 3538948
  187.3 9.2 %copy-start.7 = (f32[2,32,16,8,8]{3,4,2,1,0:T(8,128)S(1)}, f32[2,32,16,8,8]{3,4,2,1,0:T(8,128)}, u32[]{:S(2)}) copy-start(f32[2,32,16,8,8]{3,4,2,1,0:T(8,128)} %get-tuple-element.33) | copy-start | bytes 786436
  196.5 7.4 %copy-start.8 = (f32[2,32,16,8]{3,2,1,0:T(8,128)}, f32[2,32,16,8]{3,2,1,0:T(8,128)S(1)}, u32[]{:S(2)}) copy-start(f32[2,32,16,8]{3,2,1,0:T(8,128)S(1)} %get-tuple-element.34) | copy-start | bytes 98308
  210.3 21.1 %all-to-all-start.6 = ((bf16[2,8,32,1152]{3,2,0,1:T(8,128)(2,1)}), bf16[2,8,32,1152]{3,2,0,1:T(8,128)(2,1)}, u32[]{:S(2)}, u32[]{:S(2)}) async-start(bf16[2,8,32,1152]{3,2,0,1:T(8,128)(2,1)} %reshape.206), calls=%async_computation.6 | async-start | bytes 2359296 | tf_op jit(solution)/shard_map/all_to_all | solution.py:117
  231.4 21.1 %all-to-all-start.5 = ((bf16[2,8,32,1152]{3,2,0,1:T(8,128)(2,1)}), bf16[2,8,32,1152]{3,2,0,1:T(8,128)(2,1)}, u32[]{:S(2)}, u32[]{:S(2)}) async-start(bf16[2,8,32,1152]{3,2,0,1:T(8,128)(2,1)} %reshape.205), calls=%async_computation.5 | async-start | bytes 2359296 | tf_op jit(solution)/shard_map/all_to_all | solution.py:116
  252.5 21.1 %all-to-all-start.7 = ((bf16[2,8,32,1152]{3,2,0,1:T(8,128)(2,1)}), bf16[2,8,32,1152]{3,2,0,1:T(8,128)(2,1)}, u32[]{:S(2)}, u32[]{:S(2)}) async-start(bf16[2,8,32,1152]{3,2,0,1:T(8,128)(2,1)} %reshape.207), calls=%async_computation.7 | async-start | bytes 2359296 | tf_op jit(solution)/shard_map/all_to_all | solution.py:118
  256.7 62.3 %all-reduce.2.cloned.1.call-start = ((), (), s32[]{:S(2)}) async-start(), calls=%async_computation.9 | async-start | bytes 2359296 | tf_op jit(solution)/shard_map/psum | solution.py:74
  273.5 2.5 copy-start.2
Sparse Core Ops, SparseCore 0:
  149.4 60.1 reduce-scatter.3
  259.9 59.0 all-reduce.1
